TPU v7x, 32 devices: a whole 2x2x4 slice. The times are simulated.
32 devices in a mesh: groups: 2 (over x), gx: 8 (over z, y), gy: 2 (over core).
Axes of the slice: x: 2, y: 2, z: 4, core: 2. Of those that a mesh axis runs over, the one named last changes fastest.
Arguments:
- source: float32 [2, 3, 2, 32, 64, 256], P('groups', None, None, 'gx', 'gy'), parts along dimension 0, may hold values from -12 to 12
- permittivity: float32 [6, 32, 64, 256], P('groups', 'gx', 'gy'), parts along dimension 0, may hold values from 1 to 12
- frequency: float32 [1], replicated, may hold values from 0.25 to 0.6
Outputs:
- solution: float32 [2, 3, 2, 32, 64, 256], P('groups', None, None, 'gx', 'gy'), parts along dimension 0
- residual: float32 [2, 3, 2, 32, 64, 256], P('groups', None, None, 'gx', 'gy'), parts along dimension 0
There are 2 independent parts, one for each index of `groups`. A program takes and returns all parts, laid end to end along the dimension named above; an argument that names none is the same for every part. Nothing has to cross between parts.
All inputs are finite; a program needn't handle non-finite values.
Results may differ from a plain program's by a relative error of at most 0.0003.
Values sent between devices are 32-bit elements; how exact they have to be, the bound alone decides.
A program may use at most 64 MiB of HBM per device.

v0:
```python
import jax
import jax.numpy as jnp
from jax import lax
from jax.sharding import PartitionSpec as P

NZ = 256
PML = 8
ITERS = 3
pml_strength = 2.0


def shifted(array, axis, by):
    devices = lax.axis_size(axis)
    pairs = [(i, i + by) for i in range(devices) if 0 <= i + by < devices]
    return lax.ppermute(array, axis, pairs)


def stretch(points, length, frequency):
    inside = jnp.maximum(jnp.maximum(PML - points, points - (length - PML)), 0.0) / PML
    damping = pml_strength * inside**3 / frequency[:, None]
    factor = 1.0 / (1.0 + damping * damping)
    return jnp.stack([factor, -damping * factor], axis=1)


def orient(coefficient, dimension):
    target = [coefficient.shape[0], 2, 1, 1, 1]
    target[dimension] = coefficient.shape[2]
    return coefficient.reshape(target)


def times_coef(values, coefficient):
    real_part = values[:, 0] * coefficient[:, 0] - values[:, 1] * coefficient[:, 1]
    imag_part = values[:, 0] * coefficient[:, 1] + values[:, 1] * coefficient[:, 0]
    return jnp.stack([real_part, imag_part], axis=1)


def curl_forward(extended, front_x, front_y, front_z):
    centre = extended[:, :, :, :-1, :-1]

    def step_x(component):
        return extended[:, component, :, 1:, :-1] - centre[:, component]

    def step_y(component):
        return extended[:, component, :, :-1, 1:] - centre[:, component]

    def step_z(component):
        cells = centre[:, component]
        above = jnp.concatenate([cells[..., 1:], jnp.zeros_like(cells[..., :1])], axis=-1)
        return above - cells

    curl_x = times_coef(step_y(2), front_y) - times_coef(step_z(1), front_z)
    curl_y = times_coef(step_z(0), front_z) - times_coef(step_x(2), front_x)
    curl_z = times_coef(step_x(1), front_x) - times_coef(step_y(0), front_y)
    return jnp.stack([curl_x, curl_y, curl_z], axis=1)


def curl_backward(padded, back_x, back_y, back_z):
    centre = padded[:, :, :, 1:, 1:]

    def step_x(component):
        return centre[:, component] - padded[:, component, :, :-1, 1:]

    def step_y(component):
        return centre[:, component] - padded[:, component, :, 1:, :-1]

    def step_z(component):
        cells = centre[:, component]
        below = jnp.concatenate([jnp.zeros_like(cells[..., :1]), cells[..., :-1]], axis=-1)
        return cells - below

    out_x = times_coef(step_y(2), back_y) - times_coef(step_z(1), back_z)
    out_y = times_coef(step_z(0), back_z) - times_coef(step_x(2), back_x)
    out_z = times_coef(step_x(1), back_x) - times_coef(step_y(0), back_y)
    return jnp.stack([out_x, out_y, out_z], axis=1)


def scaled(values, number):
    real_scale = number[0].reshape(-1, 1, 1, 1, 1)
    imag_scale = number[1].reshape(-1, 1, 1, 1, 1)
    real_part = values[:, :, 0] * real_scale - values[:, :, 1] * imag_scale
    imag_part = values[:, :, 0] * imag_scale + values[:, :, 1] * real_scale
    return jnp.stack([real_part, imag_part], axis=2)


def product(left, right):
    real_part = jnp.sum(
        left[:, :, 0] * right[:, :, 0] + left[:, :, 1] * right[:, :, 1], axis=(1, 2, 3, 4)
    )
    imag_part = jnp.sum(
        left[:, :, 0] * right[:, :, 1] - left[:, :, 1] * right[:, :, 0], axis=(1, 2, 3, 4)
    )
    return jnp.stack([real_part, imag_part])


def complex_times(first, other):
    return jnp.stack(
        [first[0] * other[0] - first[1] * other[1], first[0] * other[1] + first[1] * other[0]]
    )


def complex_ratio(first, other):
    modulus = other[0] * other[0] + other[1] * other[1]
    return (
        jnp.stack(
            [first[0] * other[0] + first[1] * other[1], first[1] * other[0] - first[0] * other[1]]
        )
        / modulus
    )


def grid_points(start, first, count):
    return (start + jnp.arange(first, count, dtype=jnp.int32)).astype(jnp.float32)


def body(source, permittivity, frequency):
    cells_x = source.shape[3]
    cells_y = source.shape[4]
    total_x = cells_x * lax.axis_size("gx")
    total_y = cells_y * lax.axis_size("gy")
    index_x = lax.axis_index("gx")
    index_y = lax.axis_index("gy")
    margin = 0
    front_x = orient(
        stretch(grid_points(index_x * cells_x, -margin, cells_x) + 0.5, total_x, frequency), 2
    )
    front_y = orient(
        stretch(grid_points(index_y * cells_y, -margin, cells_y) + 0.5, total_y, frequency), 3
    )
    back_x = orient(stretch(grid_points(index_x * cells_x, 0, cells_x), total_x, frequency), 2)
    back_y = orient(stretch(grid_points(index_y * cells_y, 0, cells_y), total_y, frequency), 3)
    z_points = grid_points(0, 0, NZ)
    front_z = orient(stretch(z_points + 0.5, NZ, frequency), 4)
    back_z = orient(stretch(z_points, NZ, frequency), 4)
    material = (frequency * frequency).reshape(-1, 1, 1, 1, 1, 1) * permittivity[None, :, None]

    def operate(values):
        above_x = shifted(values[:, :, :, :1], "gx", -1)
        above_y = shifted(values[:, :, :, :, :1], "gy", -1)
        extended = jnp.concatenate([values, above_x], axis=3)
        side_cells = jnp.concatenate([above_y, jnp.zeros_like(above_y[:, :, :, :1])], axis=3)
        extended = jnp.concatenate([extended, side_cells], axis=4)
        rotated = curl_forward(extended, front_x, front_y, front_z)
        below_x = shifted(rotated[:, :, :, -1:], "gx", 1)
        below_y = shifted(rotated[:, :, :, :, -1:], "gy", 1)
        padded = jnp.concatenate([below_x, rotated], axis=3)
        side_cells = jnp.concatenate([jnp.zeros_like(below_y[:, :, :, :1]), below_y], axis=3)
        padded = jnp.concatenate([side_cells, padded], axis=4)
        applied = curl_backward(padded, back_x, back_y, back_z)
        return applied - material * values

    solution = jnp.zeros_like(source)
    residual = source
    direction = source
    shadow_dot = lax.psum(product(source, residual), ("gx", "gy"))
    for iteration in range(ITERS):
        applied = operate(direction)
        step_size = complex_ratio(shadow_dot, lax.psum(product(source, applied), ("gx", "gy")))
        middle = residual - scaled(applied, step_size)
        second = operate(middle)
        sums_triple = lax.psum(
            (product(second, middle), product(second, second), product(source, second)),
            ("gx", "gy"),
        )
        weight = complex_ratio(sums_triple[0], sums_triple[1])
        solution = solution + scaled(direction, step_size) + scaled(middle, weight)
        residual = middle - scaled(second, weight)
        if iteration + 1 < ITERS:
            shadow_next = -complex_times(weight, sums_triple[2])
            momentum = complex_times(
                complex_ratio(shadow_next, shadow_dot), complex_ratio(step_size, weight)
            )
            direction = residual + scaled(direction - scaled(applied, weight), momentum)
            shadow_dot = shadow_next
    return (solution, residual)


def solution(mesh):
    placed = (P("groups", None, None, "gx", "gy", None), P("groups", "gx", "gy", None), P())
    return jax.shard_map(
        body,
        mesh=mesh,
        in_specs=placed,
        out_specs=(
            P("groups", None, None, "gx", "gy", None),
            P("groups", None, None, "gx", "gy", None),
        ),
        check_vma=False,
    )
```

profile of v0, /device:TPU:0, one launch (start us, length us, event | category | flops | bytes accessed | tf_op | source)
XLA Modules:
  0.0 469.3 jit_solution(13969787863053648633)
XLA Ops:
  7.5 6.7 %collective-permute-done = f32[1,3,2,1,32,256]{5,4,3,2,1,0:T(8,128)S(1)} collective-permute-done((f32[1,3,2,1,32,256]{5,4,3,2,1,0:T(8,128)S(1)}, f32[1,3,2,1,32,256]{5,4,3,2,1,0:T(8,128)S(1)}, u32[]{:S(2)}, u32[]{:S(2)}) %collective-permute-start) | collective-permute-done | bytes 196640 | tf_op jit(solution)/shard_map/ppermute | solution.py:15
  17.5 5.0 %collective-permute-start.3 = (f32[1,3,2,1,32,256]{5,4,3,2,1,0:T(8,128)S(1)}, f32[1,3,2,1,32,256]{5,4,3,2,1,0:T(8,128)S(1)}, u32[]{:S(2)}, u32[]{:S(2)}) collective-permute-start(f32[1,3,2,1,32,256]{5,4,3,2,1,0:T(8,128)S(1)} %pad_maximum_fusion.33), channel_id=1, source_target_pairs={{0,2},{2,4},{4,6},{6,8},{8,10},{10,12},{12,14},{1,3},{3,5},{5,7},{... | collective-permute-start | bytes 589832 | tf_op jit(solution)/shard_map/ppermute | solution.py:15
  22.5 3.6 collective-permute-done.3
  31.1 31.3 %all-reduce.39 = (f32[2,1]{1,0:T(2,128)S(1)}, f32[2,1]{1,0:T(2,128)S(1)}) all-reduce(f32[2,1]{1,0:T(2,128)S(1)} %pad_maximum_fusion.41, f32[2,1]{1,0:T(2,128)S(1)} %pad_maximum_fusion.42), channel_id=1, replica_groups=mesh['groups'=2,'gx'=8,'gy'=2] {'gx','gy'}, use_global_device_ids=true, to_apply=%region_2.0 | all-reduce | flops 4 | bytes 32 | tf_op jit(solution)/shard_map/psum | solution.py:154
  77.4 3.2 collective-permute-done.4
  94.9 29.5 %all-reduce.38 = (f32[2,1]{1,0:T(2,128)S(1)}, f32[2,1]{1,0:T(2,128)S(1)}, f32[2,1]{1,0:T(2,128)S(1)}) all-reduce(f32[2,1]{1,0:T(2,128)S(1)} %pad_maximum_fusion.43, f32[2,1]{1,0:T(2,128)S(1)} %pad_maximum_fusion.44, f32[2,1]{1,0:T(2,128)S(1)} %pad_maximum_fusion.45), channel_id=1, replica_groups=mesh['groups'=2,'gx'=8,'gy'=2] {'gx','gy'}, use_global_device_ids=true, to_apply=%region_8.0 | all-reduce | flops 6 | bytes 48 | tf_op jit(solution)/shard_map/psum | solution.py:160
  141.5 2.5 multiply_subtract_fusion.11
  168.3 4.2 collective-permute-done.8
  183.4 30.3 %psum.89 = f32[2,1]{1,0:T(2,128)S(1)} all-reduce(f32[2,1]{1,0:T(2,128)S(1)} %pad_maximum_fusion.46), channel_id=1, replica_groups=mesh['groups'=2,'gx'=8,'gy'=2] {'gx','gy'}, use_global_device_ids=true, to_apply=%region_17.0 | all-reduce | flops 2 | bytes 16 | tf_op jit(solution)/shard_map/psum | solution.py:157
  222.7 2.5 multiply_subtract_fusion.8
  230.0 3.4 collective-permute-done.12
  251.3 30.6 %all-reduce.37 = (f32[2,1]{1,0:T(2,128)}, f32[2,1]{1,0:T(2,128)}, f32[2,1]{1,0:T(2,128)}) all-reduce(f32[2,1]{1,0:T(2,128)} %pad_maximum_fusion.47, f32[2,1]{1,0:T(2,128)} %pad_maximum_fusion.48, f32[2,1]{1,0:T(2,128)} %pad_maximum_fusion.49), channel_id=1, replica_groups=mesh['groups'=2,'gx'=8,'gy'=2] {'gx','gy'}, use_global_device_ids=true, to_apply=%region_20.0 | all-reduce | flops 6 | bytes 48 | tf_op jit(solution)/shard_map/psum | solution.py:160
  300.1 2.5 multiply_subtract_fusion.5
  327.7 3.7 collective-permute-done.16
  342.3 3.0 add_reduce_fusion.2
  347.1 2.3 multiply_subtract_fusion.13
  349.4 30.0 %psum.93 = f32[2,1]{1,0:T(2,128)S(1)} all-reduce(f32[2,1]{1,0:T(2,128)} %pad_maximum_fusion.50), channel_id=1, replica_groups=mesh['groups'=2,'gx'=8,'gy'=2] {'gx','gy'}, use_global_device_ids=true, to_apply=%region_29.0 | all-reduce | flops 2 | bytes 16 | tf_op jit(solution)/shard_map/psum | solution.py:157
  388.2 2.5 multiply_subtract_fusion.2
  390.7 2.3 maximum_subtract_fusion.11
  395.6 2.3 multiply_subtract_fusion.9
  397.9 5.9 %collective-permute-done.20 = f32[1,3,2,1,32,256]{5,4,3,2,1,0:T(8,128)S(1)} collective-permute-done((f32[1,3,2,1,32,256]{5,4,3,2,1,0:T(8,128)S(1)}, f32[1,3,2,1,32,256]{5,4,3,2,1,0:T(8,128)S(1)}, u32[]{:S(2)}, u32[]{:S(2)}) %collective-permute-start.20) | collective-permute-done | bytes 196640 | tf_op jit(solution)/shard_map/ppermute | solution.py:15
  420.7 2.2 multiply_subtract_fusion.3
  422.9 29.5 %all-reduce.36 = (f32[2,1]{1,0:T(2,128)S(1)}, f32[2,1]{1,0:T(2,128)S(1)}) all-reduce(f32[2,1]{1,0:T(2,128)S(1)} %pad_maximum_fusion.51, f32[2,1]{1,0:T(2,128)S(1)} %pad_maximum_fusion.52), channel_id=1, replica_groups=mesh['groups'=2,'gx'=8,'gy'=2] {'gx','gy'}, use_global_device_ids=true, to_apply=%region_32.0 | all-reduce | flops 4 | bytes 32 | tf_op jit(solution)/shard_map/psum | solution.py:160
  461.4 2.6 multiply_subtract_fusion
  (463 shorter events, 127.9 us)
Async XLA Ops:
  1.6 12.5 %collective-permute-start.1 = (f32[1,3,2,4,1,256]{5,4,3,2,1,0:T(1,128)S(1)}, f32[1,3,2,4,1,256]{5,4,3,2,1,0:T(1,128)S(1)}, u32[]{:S(2)}, u32[]{:S(2)}) collective-permute-start(f32[1,3,2,4,1,256]{5,4,3,2,1,0:T(1,128)S(1)} %slice.702), channel_id=1, source_target_pairs={{1,0},{3,2},{5,4},{7,6},{9,8},{11,10},{13,12},{15,14},{17,16},{19,... | collective-permute-start | bytes 73736 | tf_op jit(solution)/shard_map/ppermute | solution.py:15
  3.9 10.2 %collective-permute-start = (f32[1,3,2,1,32,256]{5,4,3,2,1,0:T(8,128)S(1)}, f32[1,3,2,1,32,256]{5,4,3,2,1,0:T(8,128)S(1)}, u32[]{:S(2)}, u32[]{:S(2)}) collective-permute-start(f32[1,3,2,1,32,256]{5,4,3,2,1,0:T(8,128)S(1)} %slice.695), channel_id=1, source_target_pairs={{2,0},{4,2},{6,4},{8,6},{10,8},{12,10},{14,12},{3,1},{5,3},{7,5},{... | collective-permute-start | bytes 589832 | tf_op jit(solution)/shard_map/ppermute | solution.py:15
  15.4 7.2 %collective-permute-start.2 = (f32[1,3,2,4,1,256]{5,4,3,2,1,0:T(1,128)S(1)}, f32[1,3,2,4,1,256]{5,4,3,2,1,0:T(1,128)S(1)}, u32[]{:S(2)}, u32[]{:S(2)}) collective-permute-start(f32[1,3,2,4,1,256]{5,4,3,2,1,0:T(1,128)S(1)} %pad_maximum_fusion.40), channel_id=1, source_target_pairs={{0,1},{2,3},{4,5},{6,7},{8,9},{10,11},{12,13},{14,15},{16,17},{18,... | collective-permute-start | bytes 73736 | tf_op jit(solution)/shard_map/ppermute | solution.py:15
  17.5 8.7 %collective-permute-start.3 = (f32[1,3,2,1,32,256]{5,4,3,2,1,0:T(8,128)S(1)}, f32[1,3,2,1,32,256]{5,4,3,2,1,0:T(8,128)S(1)}, u32[]{:S(2)}, u32[]{:S(2)}) collective-permute-start(f32[1,3,2,1,32,256]{5,4,3,2,1,0:T(8,128)S(1)} %pad_maximum_fusion.33), channel_id=1, source_target_pairs={{0,2},{2,4},{4,6},{6,8},{8,10},{10,12},{12,14},{1,3},{3,5},{5,7},{... | collective-permute-start | bytes 589832 | tf_op jit(solution)/shard_map/ppermute | solution.py:15
  73.0 7.6 %collective-permute-start.4 = (f32[1,3,2,1,32,256]{5,4,3,2,1,0:T(8,128)S(1)}, f32[1,3,2,1,32,256]{5,4,3,2,1,0:T(8,128)S(1)}, u32[]{:S(2)}, u32[]{:S(2)}) collective-permute-start(f32[1,3,2,1,32,256]{5,4,3,2,1,0:T(8,128)S(1)} %slice.2127), channel_id=1, source_target_pairs={{2,0},{4,2},{6,4},{8,6},{10,8},{12,10},{14,12},{3,1},{5,3},{7,5},{... | collective-permute-start | bytes 589832 | tf_op jit(solution)/shard_map/ppermute | solution.py:15
  74.3 3.1 collective-permute-start.5
  81.7 5.9 %collective-permute-start.7 = (f32[1,3,2,1,32,256]{5,4,3,2,1,0:T(8,128)S(1)}, f32[1,3,2,1,32,256]{5,4,3,2,1,0:T(8,128)S(1)}, u32[]{:S(2)}, u32[]{:S(2)}) collective-permute-start(f32[1,3,2,1,32,256]{5,4,3,2,1,0:T(8,128)S(1)} %pad_maximum_fusion.31), channel_id=1, source_target_pairs={{0,2},{2,4},{4,6},{6,8},{8,10},{10,12},{12,14},{1,3},{3,5},{5,7},{... | collective-permute-start | bytes 589832 | tf_op jit(solution)/shard_map/ppermute | solution.py:15
  83.2 4.4 collective-permute-start.6
  163.9 8.6 %collective-permute-start.8 = (f32[1,3,2,1,32,256]{5,4,3,2,1,0:T(8,128)S(1)}, f32[1,3,2,1,32,256]{5,4,3,2,1,0:T(8,128)S(1)}, u32[]{:S(2)}, u32[]{:S(2)}) collective-permute-start(f32[1,3,2,1,32,256]{5,4,3,2,1,0:T(8,128)S(1)} %slice.2170), channel_id=1, source_target_pairs={{2,0},{4,2},{6,4},{8,6},{10,8},{12,10},{14,12},{3,1},{5,3},{7,5},{... | collective-permute-start | bytes 589832 | tf_op jit(solution)/shard_map/ppermute | solution.py:15
  165.2 3.1 collective-permute-start.9
  173.6 4.9 %collective-permute-start.11 = (f32[1,3,2,1,32,256]{5,4,3,2,1,0:T(8,128)S(1)}, f32[1,3,2,1,32,256]{5,4,3,2,1,0:T(8,128)S(1)}, u32[]{:S(2)}, u32[]{:S(2)}) collective-permute-start(f32[1,3,2,1,32,256]{5,4,3,2,1,0:T(8,128)S(1)} %pad_maximum_fusion.29), channel_id=1, source_target_pairs={{0,2},{2,4},{4,6},{6,8},{8,10},{10,12},{12,14},{1,3},{3,5},{5,7},{... | collective-permute-start | bytes 589832 | tf_op jit(solution)/shard_map/ppermute | solution.py:15
  175.1 2.1 collective-permute-start.10
  225.6 7.8 %collective-permute-start.12 = (f32[1,3,2,1,32,256]{5,4,3,2,1,0:T(8,128)S(1)}, f32[1,3,2,1,32,256]{5,4,3,2,1,0:T(8,128)S(1)}, u32[]{:S(2)}, u32[]{:S(2)}) collective-permute-start(f32[1,3,2,1,32,256]{5,4,3,2,1,0:T(8,128)S(1)} %slice.2211), channel_id=1, source_target_pairs={{2,0},{4,2},{6,4},{8,6},{10,8},{12,10},{14,12},{3,1},{5,3},{7,5},{... | collective-permute-start | bytes 589832 | tf_op jit(solution)/shard_map/ppermute | solution.py:15
  226.9 3.1 collective-permute-start.13
  235.0 5.6 %collective-permute-start.15 = (f32[1,3,2,1,32,256]{5,4,3,2,1,0:T(8,128)S(1)}, f32[1,3,2,1,32,256]{5,4,3,2,1,0:T(8,128)S(1)}, u32[]{:S(2)}, u32[]{:S(2)}) collective-permute-start(f32[1,3,2,1,32,256]{5,4,3,2,1,0:T(8,128)S(1)} %pad_maximum_fusion.27), channel_id=1, source_target_pairs={{0,2},{2,4},{4,6},{6,8},{8,10},{10,12},{12,14},{1,3},{3,5},{5,7},{... | collective-permute-start | bytes 589832 | tf_op jit(solution)/shard_map/ppermute | solution.py:15
  236.5 4.0 collective-permute-start.14
  323.3 8.1 %collective-permute-start.16 = (f32[1,3,2,1,32,256]{5,4,3,2,1,0:T(8,128)S(1)}, f32[1,3,2,1,32,256]{5,4,3,2,1,0:T(8,128)S(1)}, u32[]{:S(2)}, u32[]{:S(2)}) collective-permute-start(f32[1,3,2,1,32,256]{5,4,3,2,1,0:T(8,128)S(1)} %slice.2254), channel_id=1, source_target_pairs={{2,0},{4,2},{6,4},{8,6},{10,8},{12,10},{14,12},{3,1},{5,3},{7,5},{... | collective-permute-start | bytes 589832 | tf_op jit(solution)/shard_map/ppermute | solution.py:15
  324.6 3.1 collective-permute-start.17
  333.0 5.3 %collective-permute-start.19 = (f32[1,3,2,1,32,256]{5,4,3,2,1,0:T(8,128)S(1)}, f32[1,3,2,1,32,256]{5,4,3,2,1,0:T(8,128)S(1)}, u32[]{:S(2)}, u32[]{:S(2)}) collective-permute-start(f32[1,3,2,1,32,256]{5,4,3,2,1,0:T(8,128)S(1)} %pad_maximum_fusion.25), channel_id=1, source_target_pairs={{0,2},{2,4},{4,6},{6,8},{8,10},{10,12},{12,14},{1,3},{3,5},{5,7},{... | collective-permute-start | bytes 589832 | tf_op jit(solution)/shard_map/ppermute | solution.py:15
  334.6 2.1 collective-permute-start.18
  393.0 5.0 %collective-permute-start.21 = (f32[1,3,2,4,1,256]{5,4,3,2,1,0:T(1,128)S(1)}, f32[1,3,2,4,1,256]{5,4,3,2,1,0:T(1,128)S(1)}, u32[]{:S(2)}, u32[]{:S(2)}) collective-permute-start(f32[1,3,2,4,1,256]{5,4,3,2,1,0:T(1,128)S(1)} %slice.2299), channel_id=1, source_target_pairs={{1,0},{3,2},{5,4},{7,6},{9,8},{11,10},{13,12},{15,14},{17,16},{19,... | collective-permute-start | bytes 73736 | tf_op jit(solution)/shard_map/ppermute | solution.py:15
  394.3 9.5 %collective-permute-start.20 = (f32[1,3,2,1,32,256]{5,4,3,2,1,0:T(8,128)S(1)}, f32[1,3,2,1,32,256]{5,4,3,2,1,0:T(8,128)S(1)}, u32[]{:S(2)}, u32[]{:S(2)}) collective-permute-start(f32[1,3,2,1,32,256]{5,4,3,2,1,0:T(8,128)S(1)} %slice.2295), channel_id=1, source_target_pairs={{2,0},{4,2},{6,4},{8,6},{10,8},{12,10},{14,12},{3,1},{5,3},{7,5},{... | collective-permute-start | bytes 589832 | tf_op jit(solution)/shard_map/ppermute | solution.py:15
  405.4 6.1 %collective-permute-start.22 = (f32[1,3,2,4,1,256]{5,4,3,2,1,0:T(1,128)S(1)}, f32[1,3,2,4,1,256]{5,4,3,2,1,0:T(1,128)S(1)}, u32[]{:S(2)}, u32[]{:S(2)}) collective-permute-start(f32[1,3,2,4,1,256]{5,4,3,2,1,0:T(1,128)S(1)} %pad_maximum_fusion.35), channel_id=1, source_target_pairs={{0,1},{2,3},{4,5},{6,7},{8,9},{10,11},{12,13},{14,15},{16,17},{18,... | collective-permute-start | bytes 73736 | tf_op jit(solution)/shard_map/ppermute | solution.py:15
  407.5 5.3 %collective-permute-start.23 = (f32[1,3,2,1,32,256]{5,4,3,2,1,0:T(8,128)S(1)}, f32[1,3,2,1,32,256]{5,4,3,2,1,0:T(8,128)S(1)}, u32[]{:S(2)}, u32[]{:S(2)}) collective-permute-start(f32[1,3,2,1,32,256]{5,4,3,2,1,0:T(8,128)S(1)} %pad_maximum_fusion.23), channel_id=1, source_target_pairs={{0,2},{2,4},{4,6},{6,8},{8,10},{10,12},{12,14},{1,3},{3,5},{5,7},{... | collective-permute-start | bytes 589832 | tf_op jit(solution)/shard_map/ppermute | solution.py:15
  (86 other events, 1988.6 us)
where the time goes:
time: 472 us; the launch traced here: 469 us
  blocking collectives  181 us (38%)
  between operations  99.9 us (21%)
  other arithmetic  74.5 us (16%)
  waiting for transfers between devices  43.6 us (9%)
  starting transfers between devices  38.4 us (8%)
  local copies, waits for them, and re-layouts  31.8 us (7%)
    psum x3, blocking collectives, body(): lax.psum((product(second, middle), product(second, second), product(sourc...  89.6 us
    psum x2, blocking collectives, body(): lax.psum(product(source, applied), ('gx', 'gy'))  60.3 us
    ppermute x24, waiting for transfers between devices, shifted(): return lax.ppermute(array, axis, pairs)  43.6 us
    ppermute x24, starting transfers between devices, shifted(): return lax.ppermute(array, axis, pairs)  38.4 us
    psum x1, blocking collectives, body(): shadow_dot = lax.psum(product(source, residual), ('gx', 'gy'))  31.3 us
    sub x15, other arithmetic, scaled(): real_part = values[:, :, 0] * real_scale - values[:, :, 1] * imag_scale  27.3 us
    another operation x12, other arithmetic, product(): return jnp.stack([real_part, imag_part])  17.5 us
    unnamed x173, local copies, waits for them, and re-layouts  12.9 us
  transfers between devices with their start and end apart: 24, of which 17 were waited for; matrix products, arithmetic and copies ran while one was open for 2% of the time, Pallas kernels for 0%

commit v1 on v0

--- a/solution.py
+++ b/solution.py
@@ -151,7 +151,7 @@
     solution = jnp.zeros_like(source)
     residual = source
     direction = source
-    shadow_dot = lax.psum(product(source, residual), ("gx", "gy"))
+    shadow_dot = lax.psum(lax.psum(product(source, residual), "gx"), "gy")
     for iteration in range(ITERS):
         applied = operate(direction)
         step_size = complex_ratio(shadow_dot, lax.psum(product(source, applied), ("gx", "gy")))

time: 472 us -> 494 us (1.047)
  blocking collectives: 181 us -> 201 us
    psum x2 -> x3, blocking collectives: 60.3 us -> 91.6 us  [body(): lax.psum(product(source, applied), ('gx', 'gy'))]
    psum x1 -> x2, blocking collectives: 31.3 us -> 19.6 us  [body(): shadow_dot = lax.psum(lax.psum(product(source, residual), 'gx'), 'gy')]
  transfers between devices with their start and end apart: 24 -> 24, of which waited for: 17 -> 17; matrix products, arithmetic and copies ran while one was open for 2% -> 1% of each run, Pallas kernels for 0% -> 0%
where the time goes in v1:
time: 494 us; the launch traced here: 491 us
  blocking collectives  201 us (41%)
  between operations  98 us (20%)
  other arithmetic  74.2 us (15%)
  waiting for transfers between devices  45.3 us (9%)
  starting transfers between devices  41 us (8%)
  local copies, waits for them, and re-layouts  31.6 us (6%)
    psum x3, blocking collectives, body(): lax.psum(product(source, applied), ('gx', 'gy'))  91.6 us
    psum x3, blocking collectives, body(): lax.psum((product(second, middle), product(second, second), product(sourc...  89.6 us
    ppermute x24, waiting for transfers between devices, shifted(): return lax.ppermute(array, axis, pairs)  45.3 us
    ppermute x24, starting transfers between devices, shifted(): return lax.ppermute(array, axis, pairs)  41 us
    sub x15, other arithmetic, scaled(): real_part = values[:, :, 0] * real_scale - values[:, :, 1] * imag_scale  27 us
    psum x2, blocking collectives, body(): shadow_dot = lax.psum(lax.psum(product(source, residual), 'gx'), 'gy')  19.6 us
    another operation x12, other arithmetic, product(): return jnp.stack([real_part, imag_part])  17.5 us
    unnamed x173, local copies, waits for them, and re-layouts  13 us
  transfers between devices with their start and end apart: 24, of which 17 were waited for; matrix products, arithmetic and copies ran while one was open for 1% of the time, Pallas kernels for 0%

profile of v1, /device:TPU:0, one launch (start us, length us, event | category | flops | bytes accessed | tf_op | source)
XLA Modules:
  0.0 490.9 jit_solution(12805036179765152023)
XLA Ops:
  7.5 6.7 %collective-permute-done = f32[1,3,2,1,32,256]{5,4,3,2,1,0:T(8,128)S(1)} collective-permute-done((f32[1,3,2,1,32,256]{5,4,3,2,1,0:T(8,128)S(1)}, f32[1,3,2,1,32,256]{5,4,3,2,1,0:T(8,128)S(1)}, u32[]{:S(2)}, u32[]{:S(2)}) %collective-permute-start) | collective-permute-done | bytes 196640 | tf_op jit(solution)/shard_map/ppermute | solution.py:15
  17.5 5.0 %collective-permute-start.3 = (f32[1,3,2,1,32,256]{5,4,3,2,1,0:T(8,128)S(1)}, f32[1,3,2,1,32,256]{5,4,3,2,1,0:T(8,128)S(1)}, u32[]{:S(2)}, u32[]{:S(2)}) collective-permute-start(f32[1,3,2,1,32,256]{5,4,3,2,1,0:T(8,128)S(1)} %pad_maximum_fusion.33), channel_id=1, source_target_pairs={{0,2},{2,4},{4,6},{6,8},{8,10},{10,12},{12,14},{1,3},{3,5},{5,7},{... | collective-permute-start | bytes 589832 | tf_op jit(solution)/shard_map/ppermute | solution.py:15
  22.5 3.6 collective-permute-done.3
  29.8 31.3 %psum.93 = f32[2,1]{1,0:T(2,128)S(1)} all-reduce(f32[2,1]{1,0:T(2,128)S(1)} %pad_maximum_fusion.42), channel_id=1, replica_groups=mesh['groups'=2,'gx'=8,'gy'=2] {'gx','gy'}, use_global_device_ids=true, to_apply=%region_6.0 | all-reduce | flops 2 | bytes 16 | tf_op jit(solution)/shard_map/psum | solution.py:157
  64.1 17.1 %psum.91 = f32[2,1]{1,0:T(2,128)S(1)} all-reduce(f32[2,1]{1,0:T(2,128)S(1)} %pad_maximum_fusion.41), channel_id=1, replica_groups=mesh['groups'=2,'gx'=8,'gy'=2] {'gx'}, use_global_device_ids=true, to_apply=%region_2.0 | all-reduce | flops 2 | bytes 16 | tf_op jit(solution)/shard_map/psum | solution.py:154
  82.6 2.5 psum.92
  97.3 4.7 collective-permute-done.4
  103.1 4.5 collective-permute-start.7
  118.9 29.5 %all-reduce.38 = (f32[2,1]{1,0:T(2,128)S(1)}, f32[2,1]{1,0:T(2,128)S(1)}, f32[2,1]{1,0:T(2,128)S(1)}) all-reduce(f32[2,1]{1,0:T(2,128)S(1)} %pad_maximum_fusion.43, f32[2,1]{1,0:T(2,128)S(1)} %pad_maximum_fusion.44, f32[2,1]{1,0:T(2,128)S(1)} %pad_maximum_fusion.45), channel_id=1, replica_groups=mesh['groups'=2,'gx'=8,'gy'=2] {'gx','gy'}, use_global_device_ids=true, to_apply=%region_9.0 | all-reduce | flops 6 | bytes 48 | tf_op jit(solution)/shard_map/psum | solution.py:160
  164.4 2.4 multiply_subtract_fusion.11
  190.3 4.2 collective-permute-done.8
  205.3 30.3 %psum.97 = f32[2,1]{1,0:T(2,128)S(1)} all-reduce(f32[2,1]{1,0:T(2,128)S(1)} %pad_maximum_fusion.46), channel_id=1, replica_groups=mesh['groups'=2,'gx'=8,'gy'=2] {'gx','gy'}, use_global_device_ids=true, to_apply=%region_18.0 | all-reduce | flops 2 | bytes 16 | tf_op jit(solution)/shard_map/psum | solution.py:157
  244.2 2.5 multiply_subtract_fusion.8
  251.5 3.4 collective-permute-done.12
  272.9 30.6 %all-reduce.37 = (f32[2,1]{1,0:T(2,128)}, f32[2,1]{1,0:T(2,128)}, f32[2,1]{1,0:T(2,128)}) all-reduce(f32[2,1]{1,0:T(2,128)} %pad_maximum_fusion.47, f32[2,1]{1,0:T(2,128)} %pad_maximum_fusion.48, f32[2,1]{1,0:T(2,128)} %pad_maximum_fusion.49), channel_id=1, replica_groups=mesh['groups'=2,'gx'=8,'gy'=2] {'gx','gy'}, use_global_device_ids=true, to_apply=%region_21.0 | all-reduce | flops 6 | bytes 48 | tf_op jit(solution)/shard_map/psum | solution.py:160
  321.9 2.5 multiply_subtract_fusion.5
  349.4 3.7 collective-permute-done.16
  364.1 3.0 add_reduce_fusion.2
  371.0 30.0 %psum.101 = f32[2,1]{1,0:T(2,128)S(1)} all-reduce(f32[2,1]{1,0:T(2,128)} %pad_maximum_fusion.50), channel_id=1, replica_groups=mesh['groups'=2,'gx'=8,'gy'=2] {'gx','gy'}, use_global_device_ids=true, to_apply=%region_30.0 | all-reduce | flops 2 | bytes 16 | tf_op jit(solution)/shard_map/psum | solution.py:157
  409.5 2.5 multiply_subtract_fusion.2
  419.3 5.9 %collective-permute-done.20 = f32[1,3,2,1,32,256]{5,4,3,2,1,0:T(8,128)S(1)} collective-permute-done((f32[1,3,2,1,32,256]{5,4,3,2,1,0:T(8,128)S(1)}, f32[1,3,2,1,32,256]{5,4,3,2,1,0:T(8,128)S(1)}, u32[]{:S(2)}, u32[]{:S(2)}) %collective-permute-start.20) | collective-permute-done | bytes 196640 | tf_op jit(solution)/shard_map/ppermute | solution.py:15
  442.4 2.3 multiply_subtract_fusion.3
  444.7 29.5 %all-reduce.36 = (f32[2,1]{1,0:T(2,128)S(1)}, f32[2,1]{1,0:T(2,128)S(1)}) all-reduce(f32[2,1]{1,0:T(2,128)S(1)} %pad_maximum_fusion.51, f32[2,1]{1,0:T(2,128)S(1)} %pad_maximum_fusion.52), channel_id=1, replica_groups=mesh['groups'=2,'gx'=8,'gy'=2] {'gx','gy'}, use_global_device_ids=true, to_apply=%region_33.0 | all-reduce | flops 4 | bytes 32 | tf_op jit(solution)/shard_map/psum | solution.py:160
  483.1 2.6 multiply_subtract_fusion
  (465 shorter events, 132.5 us)
Async XLA Ops:
  1.6 12.5 %collective-permute-start.1 = (f32[1,3,2,4,1,256]{5,4,3,2,1,0:T(1,128)S(1)}, f32[1,3,2,4,1,256]{5,4,3,2,1,0:T(1,128)S(1)}, u32[]{:S(2)}, u32[]{:S(2)}) collective-permute-start(f32[1,3,2,4,1,256]{5,4,3,2,1,0:T(1,128)S(1)} %slice.702), channel_id=1, source_target_pairs={{1,0},{3,2},{5,4},{7,6},{9,8},{11,10},{13,12},{15,14},{17,16},{19,... | collective-permute-start | bytes 73736 | tf_op jit(solution)/shard_map/ppermute | solution.py:15
  3.9 10.2 %collective-permute-start = (f32[1,3,2,1,32,256]{5,4,3,2,1,0:T(8,128)S(1)}, f32[1,3,2,1,32,256]{5,4,3,2,1,0:T(8,128)S(1)}, u32[]{:S(2)}, u32[]{:S(2)}) collective-permute-start(f32[1,3,2,1,32,256]{5,4,3,2,1,0:T(8,128)S(1)} %slice.695), channel_id=1, source_target_pairs={{2,0},{4,2},{6,4},{8,6},{10,8},{12,10},{14,12},{3,1},{5,3},{7,5},{... | collective-permute-start | bytes 589832 | tf_op jit(solution)/shard_map/ppermute | solution.py:15
  15.4 7.2 %collective-permute-start.2 = (f32[1,3,2,4,1,256]{5,4,3,2,1,0:T(1,128)S(1)}, f32[1,3,2,4,1,256]{5,4,3,2,1,0:T(1,128)S(1)}, u32[]{:S(2)}, u32[]{:S(2)}) collective-permute-start(f32[1,3,2,4,1,256]{5,4,3,2,1,0:T(1,128)S(1)} %pad_maximum_fusion.40), channel_id=1, source_target_pairs={{0,1},{2,3},{4,5},{6,7},{8,9},{10,11},{12,13},{14,15},{16,17},{18,... | collective-permute-start | bytes 73736 | tf_op jit(solution)/shard_map/ppermute | solution.py:15
  17.5 8.7 %collective-permute-start.3 = (f32[1,3,2,1,32,256]{5,4,3,2,1,0:T(8,128)S(1)}, f32[1,3,2,1,32,256]{5,4,3,2,1,0:T(8,128)S(1)}, u32[]{:S(2)}, u32[]{:S(2)}) collective-permute-start(f32[1,3,2,1,32,256]{5,4,3,2,1,0:T(8,128)S(1)} %pad_maximum_fusion.33), channel_id=1, source_target_pairs={{0,2},{2,4},{4,6},{6,8},{8,10},{10,12},{12,14},{1,3},{3,5},{5,7},{... | collective-permute-start | bytes 589832 | tf_op jit(solution)/shard_map/ppermute | solution.py:15
  92.9 9.1 %collective-permute-start.4 = (f32[1,3,2,1,32,256]{5,4,3,2,1,0:T(8,128)S(1)}, f32[1,3,2,1,32,256]{5,4,3,2,1,0:T(8,128)S(1)}, u32[]{:S(2)}, u32[]{:S(2)}) collective-permute-start(f32[1,3,2,1,32,256]{5,4,3,2,1,0:T(8,128)S(1)} %slice.2127), channel_id=1, source_target_pairs={{2,0},{4,2},{6,4},{8,6},{10,8},{12,10},{14,12},{3,1},{5,3},{7,5},{... | collective-permute-start | bytes 589832 | tf_op jit(solution)/shard_map/ppermute | solution.py:15
  94.2 3.1 collective-permute-start.5
  103.1 8.4 %collective-permute-start.7 = (f32[1,3,2,1,32,256]{5,4,3,2,1,0:T(8,128)S(1)}, f32[1,3,2,1,32,256]{5,4,3,2,1,0:T(8,128)S(1)}, u32[]{:S(2)}, u32[]{:S(2)}) collective-permute-start(f32[1,3,2,1,32,256]{5,4,3,2,1,0:T(8,128)S(1)} %pad_maximum_fusion.31), channel_id=1, source_target_pairs={{0,2},{2,4},{4,6},{6,8},{8,10},{10,12},{12,14},{1,3},{3,5},{5,7},{... | collective-permute-start | bytes 589832 | tf_op jit(solution)/shard_map/ppermute | solution.py:15
  107.7 3.8 collective-permute-start.6
  185.9 8.6 %collective-permute-start.8 = (f32[1,3,2,1,32,256]{5,4,3,2,1,0:T(8,128)S(1)}, f32[1,3,2,1,32,256]{5,4,3,2,1,0:T(8,128)S(1)}, u32[]{:S(2)}, u32[]{:S(2)}) collective-permute-start(f32[1,3,2,1,32,256]{5,4,3,2,1,0:T(8,128)S(1)} %slice.2170), channel_id=1, source_target_pairs={{2,0},{4,2},{6,4},{8,6},{10,8},{12,10},{14,12},{3,1},{5,3},{7,5},{... | collective-permute-start | bytes 589832 | tf_op jit(solution)/shard_map/ppermute | solution.py:15
  187.2 3.1 collective-permute-start.9
  195.6 4.9 collective-permute-start.11
  197.1 2.1 collective-permute-start.10
  247.1 7.8 %collective-permute-start.12 = (f32[1,3,2,1,32,256]{5,4,3,2,1,0:T(8,128)S(1)}, f32[1,3,2,1,32,256]{5,4,3,2,1,0:T(8,128)S(1)}, u32[]{:S(2)}, u32[]{:S(2)}) collective-permute-start(f32[1,3,2,1,32,256]{5,4,3,2,1,0:T(8,128)S(1)} %slice.2211), channel_id=1, source_target_pairs={{2,0},{4,2},{6,4},{8,6},{10,8},{12,10},{14,12},{3,1},{5,3},{7,5},{... | collective-permute-start | bytes 589832 | tf_op jit(solution)/shard_map/ppermute | solution.py:15
  248.4 3.1 collective-permute-start.13
  256.5 5.6 %collective-permute-start.15 = (f32[1,3,2,1,32,256]{5,4,3,2,1,0:T(8,128)S(1)}, f32[1,3,2,1,32,256]{5,4,3,2,1,0:T(8,128)S(1)}, u32[]{:S(2)}, u32[]{:S(2)}) collective-permute-start(f32[1,3,2,1,32,256]{5,4,3,2,1,0:T(8,128)S(1)} %pad_maximum_fusion.27), channel_id=1, source_target_pairs={{0,2},{2,4},{4,6},{6,8},{8,10},{10,12},{12,14},{1,3},{3,5},{5,7},{... | collective-permute-start | bytes 589832 | tf_op jit(solution)/shard_map/ppermute | solution.py:15
  258.0 3.9 collective-permute-start.14
  345.0 8.1 %collective-permute-start.16 = (f32[1,3,2,1,32,256]{5,4,3,2,1,0:T(8,128)S(1)}, f32[1,3,2,1,32,256]{5,4,3,2,1,0:T(8,128)S(1)}, u32[]{:S(2)}, u32[]{:S(2)}) collective-permute-start(f32[1,3,2,1,32,256]{5,4,3,2,1,0:T(8,128)S(1)} %slice.2254), channel_id=1, source_target_pairs={{2,0},{4,2},{6,4},{8,6},{10,8},{12,10},{14,12},{3,1},{5,3},{7,5},{... | collective-permute-start | bytes 589832 | tf_op jit(solution)/shard_map/ppermute | solution.py:15
  346.4 3.1 collective-permute-start.17
  354.8 5.3 %collective-permute-start.19 = (f32[1,3,2,1,32,256]{5,4,3,2,1,0:T(8,128)S(1)}, f32[1,3,2,1,32,256]{5,4,3,2,1,0:T(8,128)S(1)}, u32[]{:S(2)}, u32[]{:S(2)}) collective-permute-start(f32[1,3,2,1,32,256]{5,4,3,2,1,0:T(8,128)S(1)} %pad_maximum_fusion.25), channel_id=1, source_target_pairs={{0,2},{2,4},{4,6},{6,8},{8,10},{10,12},{12,14},{1,3},{3,5},{5,7},{... | collective-permute-start | bytes 589832 | tf_op jit(solution)/shard_map/ppermute | solution.py:15
  356.3 2.1 collective-permute-start.18
  414.4 4.9 collective-permute-start.21
  415.7 9.5 %collective-permute-start.20 = (f32[1,3,2,1,32,256]{5,4,3,2,1,0:T(8,128)S(1)}, f32[1,3,2,1,32,256]{5,4,3,2,1,0:T(8,128)S(1)}, u32[]{:S(2)}, u32[]{:S(2)}) collective-permute-start(f32[1,3,2,1,32,256]{5,4,3,2,1,0:T(8,128)S(1)} %slice.2295), channel_id=1, source_target_pairs={{2,0},{4,2},{6,4},{8,6},{10,8},{12,10},{14,12},{3,1},{5,3},{7,5},{... | collective-permute-start | bytes 589832 | tf_op jit(solution)/shard_map/ppermute | solution.py:15
  426.9 6.1 %collective-permute-start.22 = (f32[1,3,2,4,1,256]{5,4,3,2,1,0:T(1,128)S(1)}, f32[1,3,2,4,1,256]{5,4,3,2,1,0:T(1,128)S(1)}, u32[]{:S(2)}, u32[]{:S(2)}) collective-permute-start(f32[1,3,2,4,1,256]{5,4,3,2,1,0:T(1,128)S(1)} %pad_maximum_fusion.35), channel_id=1, source_target_pairs={{0,1},{2,3},{4,5},{6,7},{8,9},{10,11},{12,13},{14,15},{16,17},{18,... | collective-permute-start | bytes 73736 | tf_op jit(solution)/shard_map/ppermute | solution.py:15
  428.9 5.3 %collective-permute-start.23 = (f32[1,3,2,1,32,256]{5,4,3,2,1,0:T(8,128)S(1)}, f32[1,3,2,1,32,256]{5,4,3,2,1,0:T(8,128)S(1)}, u32[]{:S(2)}, u32[]{:S(2)}) collective-permute-start(f32[1,3,2,1,32,256]{5,4,3,2,1,0:T(8,128)S(1)} %pad_maximum_fusion.23), channel_id=1, source_target_pairs={{0,2},{2,4},{4,6},{6,8},{8,10},{10,12},{12,14},{1,3},{3,5},{5,7},{... | collective-permute-start | bytes 589832 | tf_op jit(solution)/shard_map/ppermute | solution.py:15
  (86 other events, 2204.7 us)
